TPU v7x, 256 devices: a 4x2x16 block of a 4x16x16 slice. The times are simulated.
256 devices in a mesh: rep: 2 (over y), ep: 16 (over z), tp: 8 (over x, core).
Axes of the slice: x: 4, y: 2, z: 16, core: 2. Of those that a mesh axis runs over, the one named last changes fastest.
The devices are a block of a 4x16x16 slice.
Arguments:
- residual_in: bfloat16 [4096, 4096], P(('rep', 'ep'), 'tp'), parts along dimension 0, may hold values from -3.2 to 3.2
- queries: bfloat16 [4096, 4096], P(('rep', 'ep'), 'tp'), parts along dimension 0, may hold values from -120 to 120
- key_rows: bfloat16 [4096, 256], P(('rep', 'ep')), parts along dimension 0, may hold values from -4 to 4
- value_rows: bfloat16 [4096, 256], P(('rep', 'ep')), parts along dimension 0, may hold values from -6 to 6
- seq_lengths: int32 [32], P(('rep', 'ep')), parts along dimension 0, may hold values from 64 to 128
- out_weight: bfloat16 [4096, 4096], P('tp', 'ep'), may hold values from -0.09375 to 0.09375
- norm_gain: float32 [4096], P('tp'), may hold values from 0.25 to 1.75
- expert_ids: int32 [4096, 8], P(('rep', 'ep')), parts along dimension 0, may hold values from 0 to 31, all different within a row; in each aligned block of 128 rows (0 to 127, 128 to 255, ...) at most 48 rows name the same one
- gate_probs: float32 [4096, 8], P(('rep', 'ep')), parts along dimension 0, may hold values from 0.03 to 0.5
- gate_weight: bfloat16 [32, 4096, 1536], P('ep', None, 'tp'), may hold values from -0.09375 to 0.09375
- up_weight: bfloat16 [32, 4096, 1536], P('ep', None, 'tp'), may hold values from -0.09375 to 0.09375
- down_weight: bfloat16 [32, 1536, 4096], P('ep', None, 'tp'), may hold values from -0.15625 to 0.15625
Outputs:
- layer_out: bfloat16 [4096, 4096], P(('rep', 'ep'), 'tp'), parts along dimension 0
There are 2 independent parts, one for each index of `rep`. A program takes and returns all parts, laid end to end along the dimension named above; an argument that names none is the same for every part. Nothing has to cross between parts.
Inputs may be any that keep to these rules, and one draw needn't show every extreme that they name: `expert_ids`: each row names 8 different experts. Within the rows of one sequence no expert is named by more than 48 rows, a bound that some block reaches. `seq_lengths`: each sequence's number of valid tokens.
All inputs are finite; a program needn't handle non-finite values.
Results may differ from a plain program's by a relative error of at most 0.015.
Values may be sent and summed in bfloat16 or wider, within the bound.
No kernel may reach another device: no remote copies, remote signals or barrier semaphores. Data moves between devices by JAX's collectives and lax.ppermute only.
A program may use at most 128 MiB of HBM per device.

v0:
```python
import jax
import jax.numpy as jnp
from jax import lax
from jax.sharding import PartitionSpec as P

D = 4096
HEADS = 32
KV_HEADS = 2
HEAD_DIM = 128
EPSILON = 1e-06


def in_blocks(x, dim, count):
    before, after = (x.shape[:dim], x.shape[dim + 1 :])
    return jnp.moveaxis(x.reshape(*before, count, -1, *after), dim, 0)


def sent_and_summed(x, axis, dim):
    blocks = in_blocks(x, dim, lax.axis_size(axis))
    arrived = lax.all_to_all(blocks, axis, split_axis=0, concat_axis=0, tiled=True)
    return arrived.astype(jnp.float32).sum(axis=0)


def sent_to_all(x, axis):
    count = lax.axis_size(axis)
    return lax.all_to_all(jnp.broadcast_to(x[None], (count, *x.shape)), axis, 0, 0, tiled=True)


def over_copies(x, axis):
    everything = sent_to_all(x, axis)
    return jnp.sum(everything, axis=0)


def attend(queries, key_rows, value_rows, seq_lengths):
    seq_rows = queries.shape[0]
    heads_here = queries.shape[1] // HEAD_DIM
    group_size = HEADS // KV_HEADS
    kv_column = lax.axis_index("tp") * heads_here // group_size * HEAD_DIM
    key_head = lax.dynamic_slice_in_dim(key_rows, kv_column, HEAD_DIM, 1)
    value_head = lax.dynamic_slice_in_dim(value_rows, kv_column, HEAD_DIM, 1)
    query_three = queries.reshape(seq_rows, heads_here, HEAD_DIM)
    scores = jnp.einsum(
        "qhd,kd->hqk", query_three, key_head, preferred_element_type=jnp.float32
    ) * HEAD_DIM ** (-0.5)
    positions = jnp.arange(seq_rows, dtype=jnp.int32)
    visible = (positions[None, :] <= positions[:, None]) & (positions[None, :] < seq_lengths[0])
    scores = jnp.where(visible[None, :, :], scores, jnp.float32(-1e30))
    row_peak = jnp.max(scores, axis=2, keepdims=True)
    exponent = jnp.exp(scores - row_peak)
    weights = (exponent / jnp.sum(exponent, axis=2, keepdims=True)).astype(jnp.bfloat16)
    combined = jnp.einsum("hqk,kd->qhd", weights, value_head, preferred_element_type=jnp.float32)
    return combined.astype(jnp.bfloat16).reshape(seq_rows, heads_here * HEAD_DIM)


def shards(
    residual_in,
    queries,
    key_rows,
    value_rows,
    seq_lengths,
    out_weight,
    norm_gain,
    expert_ids,
    gate_probs,
    gate_weight,
    up_weight,
    down_weight,
):
    seq_rows = residual_in.shape[0]
    attended = attend(queries, key_rows, value_rows, seq_lengths)
    projected = jnp.dot(
        attended,
        lax.all_gather(out_weight, "ep", axis=1, tiled=True),
        preferred_element_type=jnp.float32,
    )
    head_total = sent_and_summed(projected.astype(jnp.bfloat16), "tp", 1)
    residual = (residual_in.astype(jnp.float32) + head_total).astype(jnp.bfloat16)
    residual_wide = residual.astype(jnp.float32)
    square_sum = over_copies(jnp.sum(residual_wide * residual_wide, axis=1), "tp")
    mean_square = square_sum / D
    normed = (residual_wide * lax.rsqrt(mean_square + EPSILON)[:, None] * norm_gain).astype(
        jnp.bfloat16
    )
    top_count = expert_ids.shape[1]
    local_experts = gate_weight.shape[0]
    ep_count = lax.axis_size("ep")
    expert_count = local_experts * ep_count
    capacity = min(seq_rows, 3 * seq_rows * top_count // (2 * expert_count))
    flat_ids = expert_ids.reshape(-1)
    one_hot = (flat_ids[:, None] == jnp.arange(expert_count, dtype=jnp.int32)[None, :]).astype(
        jnp.int32
    )
    earlier = jnp.cumsum(one_hot, axis=0) - one_hot
    slot_rank = jnp.sum(earlier * one_hot, axis=1)
    target = flat_ids * capacity + slot_rank
    pair_token = jnp.arange(seq_rows * top_count, dtype=jnp.int32) // top_count
    token_of = jnp.zeros((expert_count * capacity,), jnp.int32).at[target].set(pair_token)
    filled = jnp.zeros((expert_count * capacity,), jnp.bool_).at[target].set(True)
    taken = jnp.where(
        filled[:, None], jnp.take(normed, token_of, axis=0), jnp.zeros((), normed.dtype)
    )
    arrived = lax.all_gather(
        lax.all_to_all(
            taken.reshape(ep_count, local_experts, capacity, normed.shape[1]),
            "ep",
            split_axis=0,
            concat_axis=0,
            tiled=True,
        ),
        "tp",
        axis=3,
        tiled=True,
    )
    gate_val = jnp.einsum(
        "secd,edf->secf", arrived, gate_weight, preferred_element_type=jnp.float32
    )
    up_val = jnp.einsum("secd,edf->secf", arrived, up_weight, preferred_element_type=jnp.float32)
    active = (jax.nn.silu(gate_val) * up_val).astype(jnp.bfloat16)
    hidden_all = lax.all_gather(active, "tp", axis=3, tiled=True)
    produced = jnp.einsum(
        "secf,efd->secd", hidden_all, down_weight, preferred_element_type=jnp.float32
    )
    returned_rows = lax.all_to_all(
        produced.astype(jnp.bfloat16), "ep", split_axis=0, concat_axis=0, tiled=True
    ).astype(produced.dtype)
    flat_back = returned_rows.reshape(expert_count * capacity, returned_rows.shape[3])
    picked = jnp.take(flat_back, target, axis=0).reshape(seq_rows, top_count, flat_back.shape[1])
    mixture = jnp.einsum("tk,tkd->td", gate_probs, picked)
    return (residual_wide + mixture).astype(jnp.bfloat16)


def solution(mesh):
    return jax.shard_map(
        shards,
        mesh=mesh,
        in_specs=(
            P(("rep", "ep"), "tp"),
            P(("rep", "ep"), "tp"),
            P(("rep", "ep"), None),
            P(("rep", "ep"), None),
            P(("rep", "ep")),
            P("tp", "ep"),
            P("tp"),
            P(("rep", "ep"), None),
            P(("rep", "ep"), None),
            P("ep", None, "tp"),
            P("ep", None, "tp"),
            P("ep", None, "tp"),
        ),
        out_specs=P(("rep", "ep"), "tp"),
        check_vma=False,
    )
```

profile of v0, /device:TPU:40, one launch (start us, length us, event | category | flops | bytes accessed | tf_op | source)
XLA Modules:
  0.0 519.2 jit_solution(854462992069098859)
XLA Ops:
  6.6 0.7 all-gather.4.cloned.1.call-update
  8.1 0.8 copy.73
  8.9 0.1 eq.26
  9.0 9.0 %reduce-window.6 = s32[32,8,128]{2,1,0:T(8,128)S(1)} reduce-window(s32[32,8,128]{2,1,0:T(8,128)S(1)} %fusion.40, s32[]{:T(128)} %constant.48.clone.1), window={size=1x1x128 pad=0_0x0_0x127_0}, to_apply=%region_3.4 | reduce-window | flops 4161536 | bytes 262148 | tf_op jit(solution)/shard_map/reduce-window
  18.0 0.1 slice.12
  18.1 0.1 copy.75
  18.4 0.1 fusion.41
  18.5 1.2 fusion.65
  19.7 1.8 fusion.27
  21.5 1.9 convolution_convert_fusion.1
  23.4 0.1 broadcast_add_fusion
  23.5 91.3 %all-gather.4.cloned.1.call-done = bf16[512,4096]{1,0:T(8,128)(2,1)} async-done(((bf16[512,256]{1,0:T(8,128)(2,1)}), bf16[512,4096]{1,0:T(8,128)(2,1)}) %all-gather.4.cloned.1.call-update) | async-done | bytes 4194320 | tf_op jit(solution)/shard_map/all_gather | solution.py:73
  114.8 3.0 convolution_convert_fusion
  117.8 1.1 copy.112
  119.0 4.5 all-to-all-start
  123.5 0.1 reshape.144
  123.6 0.1 copy.79
  123.7 0.1 mul.71
  123.9 4.3 scatter_custom_fusion.1
  128.3 11.1 %all-to-all-done = bf16[8,128,512]{2,1,0:T(8,128)(2,1)} async-done(((bf16[8,128,512]{2,1,0:T(8,128)(2,1)}), bf16[8,128,512]{2,1,0:T(8,128)(2,1)}, u32[]{:S(2)}, u32[]{:S(2)}) %all-to-all-start) | async-done | bytes 1048608 | tf_op jit(solution)/shard_map/all_to_all | solution.py:20
  139.4 1.4 convert_reduce_fusion
  140.8 1.0 fusion.31
  141.8 0.6 broadcast_in_dim.87
  142.4 3.5 all-to-all-start.1
  146.0 0.1 broadcast_in_dim.85
  146.1 4.3 scatter_custom_fusion
  150.5 0.1 broadcast_in_dim.82
  150.6 0.3 all-to-all-done.1
  150.9 0.1 fusion.33
  151.0 5.4 %gather_fusion = bf16[1536,512]{1,0:T(8,128)(2,1)} fusion(bf16[128,512]{1,0:T(8,128)(2,1)S(1)} %fusion.33, s32[2048]{0:T(1024)S(1)} %pad_clamp_fusion), kind=kCustom, calls=%fused_computation | custom fusion | bytes 3151872 | tf_op jit(solution)/shard_map/jit(_take)/gather | solution.py:100
  156.5 1.7 select_select_fusion
  158.2 81.1 %all_to_all.21 = bf16[16,2,48,512]{3,2,1,0:T(8,128)(2,1)S(1)} all-to-all(bf16[16,2,48,512]{3,2,1,0:T(8,128)(2,1)S(1)} %select_select_fusion), channel_id=1, replica_groups=mesh['rep'=2,'ep'=16,'tp'=8] {'ep'}, dimensions={0} | all-to-all | bytes 3145728 | tf_op jit(solution)/shard_map/all_to_all | solution.py:103
  239.3 1.3 copy.81
  240.6 0.2 all-gather.8.cloned.1.call-start
  240.9 68.9 %all-gather.6.cloned.1.call-done = bf16[16,2,48,4096]{3,2,0,1:T(8,128)(2,1)} async-done(((bf16[16,2,48,512]{3,2,0,1:T(8,128)(2,1)}), bf16[16,2,48,4096]{3,2,0,1:T(8,128)(2,1)}) %all-gather.6.cloned.1.call-update) | async-done | bytes 12582928 | tf_op jit(solution)/shard_map/all_gather | solution.py:102
  309.8 7.5 %fusion.6 = f32[2,16,48,192]{3,2,1,0:T(8,128)S(1)} fusion(bf16[16,2,48,4096]{3,2,0,1:T(8,128)(2,1)} %all-gather.6.cloned.1.call-done, bf16[2,4096,192]{1,2,0:T(8,128)(2,1)} %param.21), kind=kOutput, calls=%fused_computation.11 | convolution fusion | flops 2415919104 | bytes 16908288 | tf_op jit(solution)/shard_map/secd,edf->secf/dot_general | solution.py:114
  317.3 9.1 %fusion.14 = bf16[16,2,48,192]{3,2,0,1:T(8,128)(2,1)} fusion(f32[2,16,48,192]{3,2,1,0:T(8,128)S(1)} %fusion.6, bf16[16,2,48,4096]{3,2,0,1:T(8,128)(2,1)} %all-gather.6.cloned.1.call-done, bf16[2,4096,192]{1,2,0:T(8,128)(2,1)S(1)} %copy-done.4), kind=kOutput, calls=%fused_computation.19 | convolution fusion | flops 2417688576 | bytes 17498112 | tf_op jit(solution)/shard_map/secd,edf->secf/dot_general | solution.py:117
  326.3 3.2 copy.82
  329.6 73.9 %all-gather.8.cloned.1.call-done = bf16[16,2,48,1536]{2,0,1,3:T(8,128)(2,1)} async-done(((bf16[16,2,48,192]{2,0,1,3:T(8,128)(2,1)}), bf16[16,2,48,1536]{2,0,1,3:T(8,128)(2,1)}) %all-gather.8.cloned.1.call-update) | async-done | bytes 4718608 | tf_op jit(solution)/shard_map/all_gather | solution.py:119
  403.5 10.3 %fusion.18 = bf16[16,2,48,512]{3,2,0,1:T(8,128)(2,1)} fusion(bf16[2,1536,512]{2,1,0:T(8,128)(2,1)S(1)} %copy-done, bf16[16,2,48,1536]{2,0,1,3:T(8,128)(2,1)} %all-gather.8.cloned.1.call-done), kind=kOutput, calls=%fused_computation.26 | convolution fusion | flops 2416705536 | bytes 9437184 | tf_op jit(solution)/shard_map/secf,efd->secd/dot_general | solution.py:120
  413.9 2.7 copy.84
  416.6 12.5 %all-to-all-start.3 = ((bf16[16,2,48,512]{3,2,1,0:T(8,128)(2,1)}), bf16[16,2,48,512]{3,2,1,0:T(8,128)(2,1)}, u32[]{:S(2)}, u32[]{:S(2)}) async-start(bf16[16,2,48,512]{3,2,1,0:T(8,128)(2,1)} %copy.84), calls=%async_computation.3 | async-start | bytes 3145728 | tf_op jit(solution)/shard_map/all_to_all | solution.py:123
  429.2 0.1 copy.78
  429.4 0.1 copy.89
  429.5 74.0 %all-to-all-done.3 = bf16[16,2,48,512]{3,2,1,0:T(8,128)(2,1)} async-done(((bf16[16,2,48,512]{3,2,1,0:T(8,128)(2,1)}), bf16[16,2,48,512]{3,2,1,0:T(8,128)(2,1)}, u32[]{:S(2)}, u32[]{:S(2)}) %all-to-all-start.3) | async-done | bytes 1572896 | tf_op jit(solution)/shard_map/all_to_all | solution.py:123
  503.5 6.7 %gather_fusion.1 = bf16[1024,512]{1,0:T(8,128)(2,1)} fusion(bf16[1536,512]{1,0:T(8,128)(2,1)} %bitcast.101, s32[1024]{0:T(1024)S(1)} %broadcast_clamp_fusion), kind=kCustom, calls=%fused_computation.1 | custom fusion | bytes 2101248 | tf_op jit(solution)/shard_map/jit(_take)/gather | solution.py:127
  510.2 1.7 fusion.8
  512.0 0.7 fusion.34
  (35 shorter events, 0.6 us)
Async XLA Ops:
  6.5 397.0 %copy-start = (bf16[2,1536,512]{2,1,0:T(8,128)(2,1)S(1)}, bf16[2,1536,512]{2,1,0:T(8,128)(2,1)}, u32[]{:S(2)}) copy-start(bf16[2,1536,512]{2,1,0:T(8,128)(2,1)} %param.23) | copy-start | bytes 9437188
  6.6 14.9 %copy-start.5 = (bf16[128,256]{1,0:T(8,128)(2,1)S(1)}, bf16[128,256]{1,0:T(8,128)(2,1)}, u32[]{:S(2)}) copy-start(bf16[128,256]{1,0:T(8,128)(2,1)} %param.15) | copy-start | bytes 196612
  6.6 108.3 %all-gather.4.cloned.1.call-start = ((), (), s32[]{:S(2)}) async-start(), calls=%async_computation.4 | async-start | bytes 4456448 | tf_op jit(solution)/shard_map/all_gather | solution.py:73
  117.8 5.7 %copy-start.1 = (s32[128,8]{0,1:T(8,128)S(1)}, s32[128,8]{0,1:T(8,128)}, u32[]{:S(2)}) copy-start(s32[128,8]{0,1:T(8,128)} %param.19) | copy-start | bytes 12292
  119.0 32.0 %copy-start.3 = (f32[512]{0:T(512)S(1)}, f32[512]{0:T(512)}, u32[]{:S(2)}) copy-start(f32[512]{0:T(512)} %param.18) | copy-start | bytes 6148
  119.0 20.4 %all-to-all-start = ((bf16[8,128,512]{2,1,0:T(8,128)(2,1)}), bf16[8,128,512]{2,1,0:T(8,128)(2,1)}, u32[]{:S(2)}, u32[]{:S(2)}) async-start(bf16[8,128,512]{2,1,0:T(8,128)(2,1)} %bitcast.125), calls=%async_computation | async-start | bytes 2097152 | tf_op jit(solution)/shard_map/all_to_all | solution.py:20
  142.4 8.5 %all-to-all-start.1 = ((f32[8,1,128]{2,1,0:T(1,128)}), f32[8,1,128]{2,1,0:T(1,128)S(1)}, u32[]{:S(2)}, u32[]{:S(2)}) async-start(f32[8,1,128]{2,1,0:T(1,128)} %broadcast_in_dim.87), calls=%async_computation.1 | async-start | bytes 8192 | tf_op jit(solution)/shard_map/all_to_all | solution.py:26
  145.9 163.8 %all-gather.6.cloned.1.call-start = ((), (), s32[]{:S(2)}) async-start(), calls=%async_computation.5 | async-start | bytes 14155776 | tf_op jit(solution)/shard_map/all_gather | solution.py:102
  240.6 162.9 %all-gather.8.cloned.1.call-start = ((), (), s32[]{:S(2)}) async-start(), calls=%async_computation.6 | async-start | bytes 14155776 | tf_op jit(solution)/shard_map/all_gather | solution.py:119
  309.8 7.5 %copy-start.4 = (bf16[2,4096,192]{1,2,0:T(8,128)(2,1)S(1)}, bf16[2,4096,192]{1,2,0:T(8,128)(2,1)}, u32[]{:S(2)}) copy-start(bf16[2,4096,192]{1,2,0:T(8,128)(2,1)} %param.22) | copy-start | bytes 9437188
  416.6 12.8 %copy-start.2 = (f32[128,8]{0,1:T(8,128)S(1)}, f32[128,8]{0,1:T(8,128)}, u32[]{:S(2)}) copy-start(f32[128,8]{0,1:T(8,128)} %param.20) | copy-start | bytes 12292
  416.6 87.0 %all-to-all-start.3 = ((bf16[16,2,48,512]{3,2,1,0:T(8,128)(2,1)}), bf16[16,2,48,512]{3,2,1,0:T(8,128)(2,1)}, u32[]{:S(2)}, u32[]{:S(2)}) async-start(bf16[16,2,48,512]{3,2,1,0:T(8,128)(2,1)} %copy.84), calls=%async_computation.3 | async-start | bytes 3145728 | tf_op jit(solution)/shard_map/all_to_all | solution.py:123
Sparse Core Ops, SparseCore 0:
  9.1 105.6 all-gather.3
  240.8 68.9 all-gather.5
  329.7 73.7 all-gather.7
where the time goes:
time: 520 us; the launch traced here: 519 us
  waiting for transfers between devices  320 us (62%)
  blocking collectives  81.1 us (16%)
  matrix products  36.5 us (7%)
  local copies, waits for them, and re-layouts  31.8 us (6%)
  starting transfers between devices  20.9 us (4%)
  other arithmetic  14.3 us (3%)
  between operations  14.2 us (3%)
    all_gather x1, waiting for transfers between devices, shards(): lax.all_gather(out_weight, 'ep', axis=1, tiled=True)  91.3 us
    all_to_all x1, blocking collectives, shards(): lax.all_to_all(taken.reshape(ep_count, local_experts, capacity, normed.sh...  81.1 us
    all_to_all x1, waiting for transfers between devices, shards(): lax.all_to_all(produced.astype(jnp.bfloat16), 'ep', split_axis=0, concat_...  74 us
    all_gather x1, waiting for transfers between devices, shards(): hidden_all = lax.all_gather(active, 'tp', axis=3, tiled=True)  73.9 us
    all_gather x1, waiting for transfers between devices, shards(): lax.all_gather(lax.all_to_all(taken.reshape(ep_count, local_experts, capa...  68.9 us
    all_to_all x1, starting transfers between devices, shards(): lax.all_to_all(produced.astype(jnp.bfloat16), 'ep', split_axis=0, concat_...  12.5 us
    all_to_all x1, waiting for transfers between devices, sent_and_summed(): lax.all_to_all(blocks, axis, split_axis=0, concat_axis=0, tiled=True)  11.1 us
  transfers between devices with their start and end apart: 6, of which 6 were waited for; matrix products, arithmetic and copies ran while one was open for 5% of the time, Pallas kernels for 0%

commit v1 on v0

--- a/solution.py
+++ b/solution.py
@@ -8,6 +8,19 @@
 KV_HEADS = 2
 HEAD_DIM = 128
 EPSILON = 1e-06
+
+
+def ring_gather(shard, axis, dim):
+    ways = lax.axis_size(axis)
+    up = [(d, (d + 1) % ways) for d in range(ways)]
+    down = [(d, (d - 1) % ways) for d in range(ways)]
+    earlier, later = ([shard], [shard])
+    for _ in range(ways // 2):
+        earlier.append(lax.ppermute(earlier[-1], axis, up))
+    for _ in range((ways - 1) // 2):
+        later.append(lax.ppermute(later[-1], axis, down))
+    line = jnp.concatenate([*earlier[::-1], *later[1:]], axis=dim)
+    return jnp.roll(line, (lax.axis_index(axis) - ways // 2) * shard.shape[dim], axis=dim)
 
 
 def in_blocks(x, dim, count):
@@ -116,7 +129,7 @@
     )
     up_val = jnp.einsum("secd,edf->secf", arrived, up_weight, preferred_element_type=jnp.float32)
     active = (jax.nn.silu(gate_val) * up_val).astype(jnp.bfloat16)
-    hidden_all = lax.all_gather(active, "tp", axis=3, tiled=True)
+    hidden_all = ring_gather(active, "tp", 3)
     produced = jnp.einsum(
         "secf,efd->secd", hidden_all, down_weight, preferred_element_type=jnp.float32
     )

time: 520 us -> 500 us (0.962)
  waiting for transfers between devices: 320 us -> 280 us
  local copies, waits for them, and re-layouts: 31.8 us -> 47.4 us
  starting transfers between devices: 20.9 us -> 27.3 us
  matrix products: 36.5 us -> 30.5 us
    all_gather x1 -> x0, waiting for transfers between devices: 73.9 us -> none  [shards(): hidden_all = lax.all_gather(active, 'tp', axis=3, tiled=True)]
    ppermute x0 -> x7, waiting for transfers between devices: none -> 41.9 us  [the longest x4 41.6 us: ring_gather(): earlier.append(lax.ppermute(earlier[-1], axis, up))]
    concatenate x0 -> x1, local copies, waits for them, and re-layouts: none -> 17.8 us  [ring_gather(): jnp.roll(line, (lax.axis_index(axis) - ways // 2) * shard.shape[dim], axi...]
    all_to_all x1, waiting for transfers between devices: 74 us -> 64.9 us  [shards(): lax.all_to_all(produced.astype(jnp.bfloat16), 'ep', split_axis=0, concat_...]
    ppermute x0 -> x7, starting transfers between devices: none -> 6.72 us  [the longest x3 6.41 us: ring_gather(): later.append(lax.ppermute(later[-1], axis, down))]
    dot_general x1, matrix products: 10.3 us -> 5.14 us  [shards(): jnp.einsum('secf,efd->secd', hidden_all, down_weight, preferred_element_t...]
  transfers between devices with their start and end apart: 6 -> 12, of which waited for: 6 -> 10; matrix products, arithmetic and copies ran while one was open for 5% -> 5% of each run, Pallas kernels for 0% -> 0%
where the time goes in v1:
time: 500 us; the launch traced here: 495 us
  waiting for transfers between devices  280 us (56%)
  blocking collectives  81.1 us (16%)
  local copies, waits for them, and re-layouts  47.4 us (9%)
  matrix products  30.5 us (6%)
  starting transfers between devices  27.3 us (5%)
  between operations  14.6 us (3%)
  other arithmetic  14.3 us (3%)
    all_gather x1, waiting for transfers between devices, shards(): lax.all_gather(out_weight, 'ep', axis=1, tiled=True)  91.3 us
    all_to_all x1, blocking collectives, shards(): lax.all_to_all(taken.reshape(ep_count, local_experts, capacity, normed.sh...  81.1 us
    all_gather x1, waiting for transfers between devices, shards(): lax.all_gather(lax.all_to_all(taken.reshape(ep_count, local_experts, capa...  69.1 us
    all_to_all x1, waiting for transfers between devices, shards(): lax.all_to_all(produced.astype(jnp.bfloat16), 'ep', split_axis=0, concat_...  64.9 us
    ppermute x4, waiting for transfers between devices, ring_gather(): earlier.append(lax.ppermute(earlier[-1], axis, up))  41.6 us
    concatenate x1, local copies, waits for them, and re-layouts, ring_gather(): jnp.roll(line, (lax.axis_index(axis) - ways // 2) * shard.shape[dim], axi...  17.8 us
    all_to_all x1, starting transfers between devices, shards(): lax.all_to_all(produced.astype(jnp.bfloat16), 'ep', split_axis=0, concat_...  12.5 us
    all_to_all x1, waiting for transfers between devices, sent_and_summed(): lax.all_to_all(blocks, axis, split_axis=0, concat_axis=0, tiled=True)  11.1 us
  transfers between devices with their start and end apart: 12, of which 10 were waited for; matrix products, arithmetic and copies ran while one was open for 5% of the time, Pallas kernels for 0%

profile of v1, /device:TPU:40, one launch (start us, length us, event | category | flops | bytes accessed | tf_op | source)
XLA Modules:
  0.0 494.6 jit_solution(16642018960827150715)
XLA Ops:
  6.6 0.7 all-gather.3.cloned.1.call-update
  8.1 0.8 copy.67
  9.0 9.0 %reduce-window.6 = s32[32,8,128]{2,1,0:T(8,128)S(1)} reduce-window(s32[32,8,128]{2,1,0:T(8,128)S(1)} %fusion.40, s32[]{:T(128)} %constant.93.clone.1), window={size=1x1x128 pad=0_0x0_0x127_0}, to_apply=%region_3.4 | reduce-window | flops 4161536 | bytes 262148 | tf_op jit(solution)/shard_map/reduce-window
  18.1 0.1 copy.69
  18.5 1.2 fusion.66
  19.7 1.8 fusion.27
  21.5 1.9 convolution_convert_fusion.1
  23.5 91.3 %all-gather.3.cloned.1.call-done = bf16[512,4096]{1,0:T(8,128)(2,1)} async-done(((bf16[512,256]{1,0:T(8,128)(2,1)}), bf16[512,4096]{1,0:T(8,128)(2,1)}) %all-gather.3.cloned.1.call-update) | async-done | bytes 4194320 | tf_op jit(solution)/shard_map/all_gather | solution.py:86
  114.8 3.0 convolution_convert_fusion
  117.8 1.1 copy.98
  119.0 4.5 all-to-all-start
  123.9 4.3 scatter_custom_fusion.1
  128.2 11.1 %all-to-all-done = bf16[8,128,512]{2,1,0:T(8,128)(2,1)} async-done(((bf16[8,128,512]{2,1,0:T(8,128)(2,1)}), bf16[8,128,512]{2,1,0:T(8,128)(2,1)}, u32[]{:S(2)}, u32[]{:S(2)}) %all-to-all-start) | async-done | bytes 1048608 | tf_op jit(solution)/shard_map/all_to_all | solution.py:33
  139.4 1.4 convert_reduce_fusion
  140.8 1.0 fusion.31
  141.8 0.6 broadcast_in_dim.87
  142.4 3.5 all-to-all-start.1
  146.1 4.3 scatter_custom_fusion
  150.6 0.3 all-to-all-done.1
  151.0 5.4 %gather_fusion = bf16[1536,512]{1,0:T(8,128)(2,1)} fusion(bf16[128,512]{1,0:T(8,128)(2,1)S(1)} %fusion.33, s32[2048]{0:T(1024)S(1)} %pad_clamp_fusion), kind=kCustom, calls=%fused_computation | custom fusion | bytes 3151872 | tf_op jit(solution)/shard_map/jit(_take)/gather | solution.py:113
  156.5 1.7 select_select_fusion
  158.2 81.1 %all_to_all.21 = bf16[16,2,48,512]{3,2,1,0:T(8,128)(2,1)S(1)} all-to-all(bf16[16,2,48,512]{3,2,1,0:T(8,128)(2,1)S(1)} %select_select_fusion), channel_id=1, replica_groups=mesh['rep'=2,'ep'=16,'tp'=8] {'ep'}, dimensions={0} | all-to-all | bytes 3145728 | tf_op jit(solution)/shard_map/all_to_all | solution.py:116
  239.3 1.3 copy.75
  240.6 69.1 %all-gather.5.cloned.1.call-done = bf16[16,2,48,4096]{3,2,0,1:T(8,128)(2,1)} async-done(((bf16[16,2,48,512]{3,2,0,1:T(8,128)(2,1)}), bf16[16,2,48,4096]{3,2,0,1:T(8,128)(2,1)}) %all-gather.5.cloned.1.call-update) | async-done | bytes 12582928 | tf_op jit(solution)/shard_map/all_gather | solution.py:115
  309.8 7.5 %fusion.6 = f32[2,16,48,192]{3,2,1,0:T(8,128)S(1)} fusion(bf16[16,2,48,4096]{3,2,0,1:T(8,128)(2,1)} %all-gather.5.cloned.1.call-done, bf16[2,4096,192]{1,2,0:T(8,128)(2,1)} %param.21), kind=kOutput, calls=%fused_computation.11 | convolution fusion | flops 2415919104 | bytes 16908288 | tf_op jit(solution)/shard_map/secd,edf->secf/dot_general | solution.py:127
  317.3 8.2 %fusion.14 = bf16[16,2,48,192]{3,2,0,1:T(8,128)(2,1)S(1)} fusion(f32[2,16,48,192]{3,2,1,0:T(8,128)S(1)} %fusion.6, bf16[16,2,48,4096]{3,2,0,1:T(8,128)(2,1)} %all-gather.5.cloned.1.call-done, bf16[2,4096,192]{1,2,0:T(8,128)(2,1)S(1)} %copy-done.8), kind=kOutput, calls=%fused_computation.19 | convolution fusion | flops 2417688576 | bytes 17498112 | tf_op jit(solution)/shard_map/secd,edf->secf/dot_general | solution.py:130
  325.5 0.3 collective-permute-start
  325.8 0.6 copy-done.1
  326.4 2.1 collective-permute-start.4
  328.5 9.7 %collective-permute-done = bf16[16,2,48,192]{3,2,0,1:T(8,128)(2,1)S(1)} collective-permute-done((bf16[16,2,48,192]{3,2,0,1:T(8,128)(2,1)S(1)}, bf16[16,2,48,192]{3,2,0,1:T(8,128)(2,1)S(1)}, u32[]{:S(2)}, u32[]{:S(2)}) %collective-permute-start) | collective-permute-done | bytes 589856 | tf_op jit(solution)/shard_map/ppermute | solution.py:19
  338.2 0.9 copy-done.2
  339.0 2.1 collective-permute-start.5
  341.2 9.6 %collective-permute-done.1 = bf16[16,2,48,192]{3,2,0,1:T(8,128)(2,1)S(1)} collective-permute-done((bf16[16,2,48,192]{3,2,0,1:T(8,128)(2,1)S(1)}, bf16[16,2,48,192]{3,2,0,1:T(8,128)(2,1)S(1)}, u32[]{:S(2)}, u32[]{:S(2)}) %collective-permute-start.1) | collective-permute-done | bytes 589856 | tf_op jit(solution)/shard_map/ppermute | solution.py:19
  350.8 0.9 copy-done.4
  351.7 2.2 collective-permute-start.6
  353.9 9.6 %collective-permute-done.2 = bf16[16,2,48,192]{3,2,0,1:T(8,128)(2,1)} collective-permute-done((bf16[16,2,48,192]{3,2,0,1:T(8,128)(2,1)S(1)}, bf16[16,2,48,192]{3,2,0,1:T(8,128)(2,1)}, u32[]{:S(2)}, u32[]{:S(2)}) %collective-permute-start.2) | collective-permute-done | bytes 589856 | tf_op jit(solution)/shard_map/ppermute | solution.py:19
  363.5 0.2 collective-permute-done.6
  363.7 12.7 %collective-permute-done.3 = bf16[16,2,48,192]{3,2,0,1:T(8,128)(2,1)} collective-permute-done((bf16[16,2,48,192]{3,2,0,1:T(8,128)(2,1)}, bf16[16,2,48,192]{3,2,0,1:T(8,128)(2,1)}, u32[]{:S(2)}, u32[]{:S(2)}) %collective-permute-start.3) | collective-permute-done | bytes 589856 | tf_op jit(solution)/shard_map/ppermute | solution.py:19
  376.5 17.8 %concatenate.6 = bf16[16,2,48,3072]{3,2,0,1:T(8,128)(2,1)} concatenate(bf16[16,2,48,192]{3,2,0,1:T(8,128)(2,1)} %collective-permute-done.3, bf16[16,2,48,192]{3,2,0,1:T(8,128)(2,1)} %collective-permute-done.2, bf16[16,2,48,192]{3,2,0,1:T(8,128)(2,1)} %copy-done.4, bf16[16,2,48,192]{3,2,0,1:T(8,128)(2,1)} %copy-done.2, bf16[16,2,48,192]{3,2,0,1:T(8,128)(2,1)} %copy-done.1, ...), dimensions={3} | concatenate | bytes 18874368 | tf_op jit(solution)/shard_map/jit(_roll_dynamic)/concatenate | solution.py:23
  394.3 5.1 %fusion.18 = bf16[16,2,48,512]{3,2,0,1:T(8,128)(2,1)S(1)} fusion(bf16[2,1536,512]{2,1,0:T(8,128)(2,1)S(1)} %copy-done, bf16[16,2,48,3072]{3,2,0,1:T(8,128)(2,1)} %concatenate.6, s32[]{:T(128)S(6)} %select_n.78), kind=kOutput, calls=%fused_computation.26 | convolution fusion | flops 2416705536 | bytes 9437188 | tf_op jit(solution)/shard_map/secf,efd->secd/dot_general | solution.py:133
  399.4 1.3 copy.76
  400.7 12.5 %all-to-all-start.3 = ((bf16[16,2,48,512]{3,2,1,0:T(8,128)(2,1)}), bf16[16,2,48,512]{3,2,1,0:T(8,128)(2,1)}, u32[]{:S(2)}, u32[]{:S(2)}) async-start(bf16[16,2,48,512]{3,2,1,0:T(8,128)(2,1)} %copy.76), calls=%async_computation.3 | async-start | bytes 3145728 | tf_op jit(solution)/shard_map/all_to_all | solution.py:136
  413.4 0.1 copy.72
  413.5 0.1 copy.81
  413.7 64.9 %all-to-all-done.3 = bf16[16,2,48,512]{3,2,1,0:T(8,128)(2,1)} async-done(((bf16[16,2,48,512]{3,2,1,0:T(8,128)(2,1)}), bf16[16,2,48,512]{3,2,1,0:T(8,128)(2,1)}, u32[]{:S(2)}, u32[]{:S(2)}) %all-to-all-start.3) | async-done | bytes 1572896 | tf_op jit(solution)/shard_map/all_to_all | solution.py:136
  478.6 6.7 %gather_fusion.1 = bf16[1024,512]{1,0:T(8,128)(2,1)} fusion(bf16[1536,512]{1,0:T(8,128)(2,1)} %bitcast.101, s32[1024]{0:T(1024)S(1)} %broadcast_clamp_fusion), kind=kCustom, calls=%fused_computation.1 | custom fusion | bytes 2101248 | tf_op jit(solution)/shard_map/jit(_take)/gather | solution.py:140
  485.3 1.7 fusion.8
  487.1 0.7 fusion.34
  (54 shorter events, 1.5 us)
Async XLA Ops:
  6.5 387.7 %copy-start = (bf16[2,1536,512]{2,1,0:T(8,128)(2,1)S(1)}, bf16[2,1536,512]{2,1,0:T(8,128)(2,1)}, u32[]{:S(2)}) copy-start(bf16[2,1536,512]{2,1,0:T(8,128)(2,1)} %param.23) | copy-start | bytes 9437188
  6.6 14.9 %copy-start.9 = (bf16[128,256]{1,0:T(8,128)(2,1)S(1)}, bf16[128,256]{1,0:T(8,128)(2,1)}, u32[]{:S(2)}) copy-start(bf16[128,256]{1,0:T(8,128)(2,1)} %param.15) | copy-start | bytes 196612
  6.6 108.3 %all-gather.3.cloned.1.call-start = ((), (), s32[]{:S(2)}) async-start(), calls=%async_computation.4 | async-start | bytes 4456448 | tf_op jit(solution)/shard_map/all_gather | solution.py:86
  117.8 5.7 %copy-start.5 = (s32[128,8]{0,1:T(8,128)S(1)}, s32[128,8]{0,1:T(8,128)}, u32[]{:S(2)}) copy-start(s32[128,8]{0,1:T(8,128)} %param.19) | copy-start | bytes 12292
  119.0 32.0 %copy-start.7 = (f32[512]{0:T(512)S(1)}, f32[512]{0:T(512)}, u32[]{:S(2)}) copy-start(f32[512]{0:T(512)} %param.18) | copy-start | bytes 6148
  119.0 20.4 %all-to-all-start = ((bf16[8,128,512]{2,1,0:T(8,128)(2,1)}), bf16[8,128,512]{2,1,0:T(8,128)(2,1)}, u32[]{:S(2)}, u32[]{:S(2)}) async-start(bf16[8,128,512]{2,1,0:T(8,128)(2,1)} %bitcast.125), calls=%async_computation | async-start | bytes 2097152 | tf_op jit(solution)/shard_map/all_to_all | solution.py:33
  142.4 8.5 %all-to-all-start.1 = ((f32[8,1,128]{2,1,0:T(1,128)}), f32[8,1,128]{2,1,0:T(1,128)S(1)}, u32[]{:S(2)}, u32[]{:S(2)}) async-start(f32[8,1,128]{2,1,0:T(1,128)} %broadcast_in_dim.87), calls=%async_computation.1 | async-start | bytes 8192 | tf_op jit(solution)/shard_map/all_to_all | solution.py:39
  145.9 163.8 %all-gather.5.cloned.1.call-start = ((), (), s32[]{:S(2)}) async-start(), calls=%async_computation.5 | async-start | bytes 14155776 | tf_op jit(solution)/shard_map/all_gather | solution.py:115
  309.8 7.5 %copy-start.8 = (bf16[2,4096,192]{1,2,0:T(8,128)(2,1)S(1)}, bf16[2,4096,192]{1,2,0:T(8,128)(2,1)}, u32[]{:S(2)}) copy-start(bf16[2,4096,192]{1,2,0:T(8,128)(2,1)} %param.22) | copy-start | bytes 9437188
  325.5 0.9 copy-start.1
  325.5 12.7 %collective-permute-start = (bf16[16,2,48,192]{3,2,0,1:T(8,128)(2,1)S(1)}, bf16[16,2,48,192]{3,2,0,1:T(8,128)(2,1)S(1)}, u32[]{:S(2)}, u32[]{:S(2)}) collective-permute-start(bf16[16,2,48,192]{3,2,0,1:T(8,128)(2,1)S(1)} %fusion.14), channel_id=1, source_target_pairs={{0,1},{1,2},{2,3},{3,4},{4,5},{5,6},{6,7},{7,0},{8,9},{9,10},{10,1... | collective-permute-start | bytes 1769480 | tf_op jit(solution)/shard_map/ppermute | solution.py:19
  326.4 11.8 %collective-permute-start.4 = (bf16[16,2,48,192]{3,2,0,1:T(8,128)(2,1)S(1)}, bf16[16,2,48,192]{3,2,0,1:T(8,128)(2,1)S(1)}, u32[]{:S(2)}, u32[]{:S(2)}) collective-permute-start(bf16[16,2,48,192]{3,2,0,1:T(8,128)(2,1)S(1)} %fusion.14), channel_id=1, source_target_pairs={{0,7},{1,0},{2,1},{3,2},{4,3},{5,4},{6,5},{7,6},{8,15},{9,8},{10,9... | collective-permute-start | bytes 1769480 | tf_op jit(solution)/shard_map/ppermute | solution.py:21
  338.2 0.9 copy-start.2
  338.2 12.6 %collective-permute-start.1 = (bf16[16,2,48,192]{3,2,0,1:T(8,128)(2,1)S(1)}, bf16[16,2,48,192]{3,2,0,1:T(8,128)(2,1)S(1)}, u32[]{:S(2)}, u32[]{:S(2)}) collective-permute-start(bf16[16,2,48,192]{3,2,0,1:T(8,128)(2,1)S(1)} %collective-permute-done), channel_id=1, source_target_pairs={{0,1},{1,2},{2,3},{3,4},{4,5},{5,6},{6,7},{7,0},{8,9},{9,10},{10,1... | collective-permute-start | bytes 1769480 | tf_op jit(solution)/shard_map/ppermute | solution.py:19
  339.0 11.7 %copy-start.3 = (bf16[16,2,48,192]{3,2,0,1:T(8,128)(2,1)}, bf16[16,2,48,192]{3,2,0,1:T(8,128)(2,1)S(1)}, u32[]{:S(2)}) copy-start(bf16[16,2,48,192]{3,2,0,1:T(8,128)(2,1)S(1)} %collective-permute-done.4) | copy-start | bytes 1769476
  339.0 11.8 %collective-permute-start.5 = (bf16[16,2,48,192]{3,2,0,1:T(8,128)(2,1)S(1)}, bf16[16,2,48,192]{3,2,0,1:T(8,128)(2,1)}, u32[]{:S(2)}, u32[]{:S(2)}) collective-permute-start(bf16[16,2,48,192]{3,2,0,1:T(8,128)(2,1)S(1)} %collective-permute-done.4), channel_id=1, source_target_pairs={{0,7},{1,0},{2,1},{3,2},{4,3},{5,4},{6,5},{7,6},{8,15},{9,8},{10,9... | collective-permute-start | bytes 1769480 | tf_op jit(solution)/shard_map/ppermute | solution.py:21
  350.8 0.9 copy-start.4
  350.8 12.7 %collective-permute-start.2 = (bf16[16,2,48,192]{3,2,0,1:T(8,128)(2,1)S(1)}, bf16[16,2,48,192]{3,2,0,1:T(8,128)(2,1)}, u32[]{:S(2)}, u32[]{:S(2)}) collective-permute-start(bf16[16,2,48,192]{3,2,0,1:T(8,128)(2,1)S(1)} %collective-permute-done.1), channel_id=1, source_target_pairs={{0,1},{1,2},{2,3},{3,4},{4,5},{5,6},{6,7},{7,0},{8,9},{9,10},{10,1... | collective-permute-start | bytes 1769480 | tf_op jit(solution)/shard_map/ppermute | solution.py:19
  351.7 12.0 %collective-permute-start.6 = (bf16[16,2,48,192]{3,2,0,1:T(8,128)(2,1)}, bf16[16,2,48,192]{3,2,0,1:T(8,128)(2,1)}, u32[]{:S(2)}, u32[]{:S(2)}) collective-permute-start(bf16[16,2,48,192]{3,2,0,1:T(8,128)(2,1)} %collective-permute-done.5), channel_id=1, source_target_pairs={{0,7},{1,0},{2,1},{3,2},{4,3},{5,4},{6,5},{7,6},{8,15},{9,8},{10,9... | collective-permute-start | bytes 1769480 | tf_op jit(solution)/shard_map/ppermute | solution.py:21
  363.5 12.9 %collective-permute-start.3 = (bf16[16,2,48,192]{3,2,0,1:T(8,128)(2,1)}, bf16[16,2,48,192]{3,2,0,1:T(8,128)(2,1)}, u32[]{:S(2)}, u32[]{:S(2)}) collective-permute-start(bf16[16,2,48,192]{3,2,0,1:T(8,128)(2,1)} %collective-permute-done.2), channel_id=1, source_target_pairs={{0,1},{1,2},{2,3},{3,4},{4,5},{5,6},{6,7},{7,0},{8,9},{9,10},{10,1... | collective-permute-start | bytes 1769480 | tf_op jit(solution)/shard_map/ppermute | solution.py:19
  400.7 12.8 %copy-start.6 = (f32[128,8]{0,1:T(8,128)S(1)}, f32[128,8]{0,1:T(8,128)}, u32[]{:S(2)}) copy-start(f32[128,8]{0,1:T(8,128)} %param.20) | copy-start | bytes 12292
  400.7 77.9 %all-to-all-start.3 = ((bf16[16,2,48,512]{3,2,1,0:T(8,128)(2,1)}), bf16[16,2,48,512]{3,2,1,0:T(8,128)(2,1)}, u32[]{:S(2)}, u32[]{:S(2)}) async-start(bf16[16,2,48,512]{3,2,1,0:T(8,128)(2,1)} %copy.76), calls=%async_computation.3 | async-start | bytes 3145728 | tf_op jit(solution)/shard_map/all_to_all | solution.py:136
Sparse Core Ops, SparseCore 0:
  9.1 105.6 all-gather.2
  240.8 68.9 all-gather.4
